TPU v7x, 32 devices: a whole 2x2x4 slice. The times are simulated.
32 devices in a mesh: ep: 4 (over z), tp: 8 (over y, x, core).
Axes of the slice: x: 2, y: 2, z: 4, core: 2. Of those that a mesh axis runs over, the one named last changes fastest.
Arguments:
- tokens: bfloat16 [384, 3072], P('ep', 'tp'), may hold values from -6 to 6
- cotangent: bfloat16 [384, 3072], P('ep', 'tp'), may hold values from -6 to 6
- expert_ids: int32 [384, 2], P('ep'), may hold values from 0 to 3, all different within a row; in each aligned block of 96 rows (0 to 95, 96 to 191, ...) at most 80 rows name the same one
- combine_weights: float32 [384, 2], P('ep'), may hold values from 0.1 to 1
- w_gate: bfloat16 [4, 3072, 8192], P('ep', None, 'tp'), may hold values from -0.15625 to 0.15625
- w_up: bfloat16 [4, 3072, 8192], P('ep', None, 'tp'), may hold values from -0.109375 to 0.109375
- w_down: bfloat16 [4, 8192, 3072], P('ep', 'tp'), may hold values from -0.09375 to 0.09375
Outputs:
- mixed: bfloat16 [384, 3072], P('ep', 'tp')
- grad_tokens: bfloat16 [384, 3072], P('ep', 'tp')
- grad_combine: float32 [384, 2], P('ep')
- grad_gate: bfloat16 [4, 3072, 8192], P('ep', 'tp')
- grad_up: bfloat16 [4, 3072, 8192], P('ep', 'tp')
- grad_down: bfloat16 [4, 8192, 3072], P('ep', None, 'tp')
Inputs may be any that keep to these rules, and one draw needn't show every extreme that they name: `expert_ids`: each row names 2 different experts. Among the 96 rows of one index of ep, no expert is named more than 80 times, and in some such blocks one expert is named exactly 80 times.
All inputs are finite; a program needn't handle non-finite values.
Results may differ from a plain program's by a relative error of at most 0.019.
Values may be sent and summed in bfloat16 or wider, within the bound.
A program may use at most 128 MiB of HBM per device.

v0:
```python
import jax
import jax.numpy as jnp
from jax import lax
from jax.sharding import PartitionSpec as P


def silu_parts(gate_pre):
    sigma = jax.nn.sigmoid(gate_pre)
    return (gate_pre * sigma, sigma * (1.0 + gate_pre * (1.0 - sigma)))


def contract_rows(left, right):
    return lax.dot_general(
        left, right, (((0,), (0,)), ((), ())), preferred_element_type=jnp.float32
    )


def contract_cols(left, right):
    return lax.dot_general(
        left, right, (((1,), (1,)), ((), ())), preferred_element_type=jnp.float32
    )


def body(tokens, cotangent, expert_ids, combine_weights, w_gate, w_up, w_down):
    groups = lax.axis_size("ep")
    tok_rows, piece_width = tokens.shape
    chosen = expert_ids.shape[1]
    capacity = tok_rows * chosen * 5 // (3 * groups)
    buffer_rows = groups * capacity
    gate_weight = w_gate[0]
    up_weight = w_up[0]
    down_weight = w_down[0]
    flat_ids = expert_ids.reshape(-1)
    onehot = (flat_ids[:, None] == jnp.arange(groups, dtype=jnp.int32)[None, :]).astype(jnp.int32)
    rank = jnp.sum((jnp.cumsum(onehot, axis=0) - onehot) * onehot, axis=1)
    slot_index = flat_ids * capacity + rank
    places = (jnp.arange(buffer_rows, dtype=jnp.int32)[:, None] == slot_index[None, :]).astype(
        jnp.bfloat16
    )
    placer = jnp.sum(
        places.reshape(buffer_rows, tok_rows, chosen).astype(jnp.float32), axis=2
    ).astype(jnp.bfloat16)
    scaled = (combine_weights[:, :, None] * cotangent[:, None, :].astype(jnp.float32)).astype(
        jnp.bfloat16
    )
    send_grad = jnp.dot(
        places, scaled.reshape(tok_rows * chosen, piece_width), preferred_element_type=jnp.float32
    ).astype(jnp.bfloat16)
    send_rows = jnp.dot(placer, tokens, preferred_element_type=jnp.float32).astype(jnp.bfloat16)
    recv_rows, recv_grad = (
        lax.all_to_all(
            send_rows.reshape(groups, capacity, piece_width),
            "ep",
            split_axis=0,
            concat_axis=0,
            tiled=True,
        ),
        lax.all_to_all(
            send_grad.reshape(groups, capacity, piece_width),
            "ep",
            split_axis=0,
            concat_axis=0,
            tiled=True,
        ),
    )
    recv_rows = recv_rows.reshape(buffer_rows, piece_width)
    piece = lax.all_gather(recv_rows, "tp", axis=1, tiled=True)
    gate_pre = jnp.dot(piece, gate_weight, preferred_element_type=jnp.float32)
    up_pre = jnp.dot(piece, up_weight, preferred_element_type=jnp.float32)
    recv_grad = recv_grad.reshape(buffer_rows, piece_width)
    active, slope = silu_parts(gate_pre)
    hidden = (active * up_pre).astype(jnp.bfloat16)
    partial_value = jnp.dot(hidden, down_weight, preferred_element_type=jnp.float32)
    out_piece = lax.psum_scatter(
        partial_value.astype(jnp.bfloat16), "tp", scatter_dimension=1, tiled=True
    )
    out_back = lax.all_to_all(
        out_piece.reshape(groups, capacity, piece_width),
        "ep",
        split_axis=0,
        concat_axis=0,
        tiled=True,
    ).reshape(buffer_rows, piece_width)
    out_tokens = (
        jnp.take(out_back, slot_index, axis=0)
        .reshape(tok_rows, chosen, piece_width)
        .astype(jnp.float32)
    )
    mixed = jnp.sum(combine_weights[:, :, None] * out_tokens, axis=1).astype(jnp.bfloat16)
    local_products = jnp.sum(cotangent.astype(jnp.float32)[:, None, :] * out_tokens, axis=2)
    grad_combine = lax.psum(local_products, "tp")
    grad_hidden = contract_cols(lax.all_gather(recv_grad, "tp", axis=1, tiled=True), down_weight)
    grad_gate_pre = (grad_hidden * up_pre * slope).astype(jnp.bfloat16)
    grad_up_pre = (grad_hidden * active).astype(jnp.bfloat16)
    input_partial = contract_cols(grad_gate_pre, gate_weight) + contract_cols(
        grad_up_pre, up_weight
    )
    input_piece = lax.psum_scatter(
        input_partial.astype(jnp.bfloat16), "tp", scatter_dimension=1, tiled=True
    )
    input_back = lax.all_to_all(
        input_piece.reshape(groups, capacity, piece_width),
        "ep",
        split_axis=0,
        concat_axis=0,
        tiled=True,
    ).reshape(buffer_rows, piece_width)
    grad_tokens = jnp.sum(
        jnp.take(input_back, slot_index, axis=0)
        .reshape(tok_rows, chosen, piece_width)
        .astype(jnp.float32),
        axis=1,
    ).astype(jnp.bfloat16)
    down_cols_out = contract_rows(
        lax.all_gather(hidden, "tp", axis=1, tiled=True), recv_grad
    ).astype(jnp.bfloat16)
    gate_rows_out = contract_rows(
        recv_rows, lax.all_gather(grad_gate_pre, "tp", axis=1, tiled=True)
    ).astype(jnp.bfloat16)
    up_rows_out = contract_rows(
        recv_rows, lax.all_gather(grad_up_pre, "tp", axis=1, tiled=True)
    ).astype(jnp.bfloat16)
    return (
        mixed,
        grad_tokens,
        grad_combine,
        gate_rows_out[None],
        up_rows_out[None],
        down_cols_out[None],
    )


def solution(mesh):
    placed = (
        P("ep", "tp"),
        P("ep", "tp"),
        P("ep", None),
        P("ep", None),
        P("ep", None, "tp"),
        P("ep", None, "tp"),
        P("ep", "tp", None),
    )
    return jax.shard_map(
        body,
        mesh=mesh,
        in_specs=placed,
        out_specs=(
            P("ep", "tp"),
            P("ep", "tp"),
            P("ep", None),
            P("ep", "tp", None),
            P("ep", "tp", None),
            P("ep", None, "tp"),
        ),
        check_vma=False,
    )
```

profile of v0, /device:TPU:0, one launch (start us, length us, event | category | flops | bytes accessed | tf_op | source)
XLA Modules:
  0.0 345.3 jit_solution(14254782053761471952)
XLA Ops:
  8.2 1.2 reduce-window.6
  9.9 1.0 mul.83
  12.3 14.8 %all_to_all.20 = bf16[4,80,384]{2,1,0:T(8,128)(2,1)} all-to-all(bf16[4,80,384]{2,1,0:T(8,128)(2,1)S(1)} %bitcast.73), channel_id=1, replica_groups=mesh['ep'=4,'tp'=8] {'ep'}, dimensions={0} | all-to-all | bytes 491520 | tf_op jit(solution)/shard_map/all_to_all | solution.py:58
  28.4 10.8 %all_to_all.21 = bf16[4,80,384]{2,1,0:T(8,128)(2,1)} all-to-all(bf16[4,80,384]{2,1,0:T(8,128)(2,1)S(1)} %bitcast.74), channel_id=1, replica_groups=mesh['ep'=4,'tp'=8] {'ep'}, dimensions={0} | all-to-all | bytes 491520 | tf_op jit(solution)/shard_map/all_to_all | solution.py:51
  39.3 14.6 %all-gather.8.cloned.1.call-done = bf16[320,3072]{1,0:T(8,128)(2,1)} async-done(((bf16[320,384]{1,0:T(8,128)(2,1)}), bf16[320,3072]{1,0:T(8,128)(2,1)}) %all-gather.8.cloned.1.call-update) | async-done | bytes 1966096 | tf_op jit(solution)/shard_map/all_gather | solution.py:92
  53.9 5.6 %fusion.3 = f32[320,1024]{1,0:T(8,128)S(1)} fusion(bf16[320,3072]{1,0:T(8,128)(2,1)} %all-gather.8.cloned.1.call-done, bf16[1,1024,3072]{2,1,0:T(8,128)(2,1)} %param.15), kind=kOutput, calls=%fused_computation.8 | convolution fusion | flops 2013265920 | bytes 9568256 | tf_op jit(solution)/shard_map/dot_general | solution.py:19
  59.5 23.8 %all-gather.6.cloned.1.call-done = bf16[320,3072]{1,0:T(8,128)(2,1)} async-done(((bf16[320,384]{1,0:T(8,128)(2,1)}), bf16[320,3072]{1,0:T(8,128)(2,1)}) %all-gather.6.cloned.1.call-update) | async-done | bytes 1966096 | tf_op jit(solution)/shard_map/all_gather | solution.py:67
  83.3 5.7 %fusion.9 = f32[320,1024]{1,0:T(8,128)S(1)} fusion(bf16[320,3072]{1,0:T(8,128)(2,1)} %all-gather.6.cloned.1.call-done, bf16[1,3072,1024]{2,1,0:T(8,128)(2,1)} %param.14), kind=kOutput, calls=%fused_computation.14 | convolution fusion | flops 2013265920 | bytes 9568256 | tf_op jit(solution)/shard_map/dot_general | solution.py:69
  89.0 6.6 %multiply_convert_fusion.1 = (bf16[320,1024]{1,0:T(8,128)(2,1)}, bf16[320,1024]{1,0:T(8,128)(2,1)S(1)}, bf16[320,1024]{1,0:T(8,128)(2,1)}) fusion(f32[320,1024]{1,0:T(8,128)S(1)} %fusion.3, f32[320,1024]{1,0:T(8,128)S(1)} %fusion.9, bf16[320,3072]{1,0:T(8,128)(2,1)S(1)} %copy-done.6, bf16[1,3072,1024]{2,1,0:T(8,128)(2,1)} %param.13), kind=kOutput, calls=%fused_computation.24 | convolution fusion | flops 2018181120 | bytes 12845056 | tf_op jit(solution)/shard_map/dot_general | solution.py:68
  95.6 7.2 %fusion.7 = f32[320,3072]{1,0:T(8,128)} fusion(bf16[320,1024]{1,0:T(8,128)(2,1)S(1)} %get-tuple-element.34, bf16[1,3072,1024]{2,1,0:T(8,128)(2,1)} %param.14), kind=kOutput, calls=%fused_computation.12 | convolution fusion | flops 2013265920 | bytes 10878976 | tf_op jit(solution)/shard_map/dot_general | solution.py:19
  102.8 6.3 %fusion.18 = bf16[320,3072]{1,0:T(8,128)(2,1)S(1)} fusion(f32[320,3072]{1,0:T(8,128)} %fusion.7, bf16[320,1024]{1,0:T(8,128)(2,1)} %get-tuple-element.33, bf16[1,3072,1024]{2,1,0:T(8,128)(2,1)} %param.13), kind=kOutput, calls=%fused_computation.21 | convolution fusion | flops 2015232000 | bytes 12845056 | tf_op jit(solution)/shard_map/dot_general | solution.py:19
  109.1 2.4 copy.51
  111.8 5.0 %fusion.21 = bf16[320,3072]{1,0:T(8,128)(2,1)S(1)} fusion(bf16[320,1024]{1,0:T(8,128)(2,1)S(1)} %copy-done.5, bf16[1,1024,3072]{2,1,0:T(8,128)(2,1)} %param.15), kind=kOutput, calls=%fused_computation.22 | convolution fusion | flops 2014248960 | bytes 8912896 | tf_op jit(solution)/shard_map/dot_general | solution.py:73
  116.8 2.4 copy.49
  121.2 32.9 %reduce-scatter.9.cloned.1.call-done = bf16[384,320]{1,0:T(8,128)(2,1)} async-done(((bf16[3072,320]{1,0:T(8,128)(2,1)}), bf16[384,320]{1,0:T(8,128)(2,1)}) %reduce-scatter.9.cloned.1.call-update) | async-done | bytes 245776
  154.1 1.8 copy.52
  155.9 4.6 %all-to-all-start.3 = ((bf16[4,80,384]{2,1,0:T(8,128)(2,1)}), bf16[4,80,384]{2,1,0:T(8,128)(2,1)S(1)}, u32[]{:S(2)}, u32[]{:S(2)}) async-start(bf16[4,80,384]{2,1,0:T(8,128)(2,1)} %bitcast.11), calls=%async_computation.3 | async-start | bytes 491520 | tf_op jit(solution)/shard_map/all_to_all | solution.py:101
  160.5 39.7 %reduce-scatter.7.cloned.1.call-done = bf16[384,320]{1,0:T(8,128)(2,1)} async-done(((bf16[3072,320]{1,0:T(8,128)(2,1)}), bf16[384,320]{1,0:T(8,128)(2,1)}) %reduce-scatter.7.cloned.1.call-update) | async-done | bytes 245776
  200.2 1.8 copy.50
  202.0 4.6 %all-to-all-start.1 = ((bf16[4,80,384]{2,1,0:T(8,128)(2,1)}), bf16[4,80,384]{2,1,0:T(8,128)(2,1)S(1)}, u32[]{:S(2)}, u32[]{:S(2)}) async-start(bf16[4,80,384]{2,1,0:T(8,128)(2,1)} %bitcast.7), calls=%async_computation.1 | async-start | bytes 491520 | tf_op jit(solution)/shard_map/all_to_all | solution.py:77
  206.7 1.0 gather_fusion.1
  207.7 7.3 %all-to-all-done.1 = bf16[4,80,384]{2,1,0:T(8,128)(2,1)S(1)} async-done(((bf16[4,80,384]{2,1,0:T(8,128)(2,1)}), bf16[4,80,384]{2,1,0:T(8,128)(2,1)S(1)}, u32[]{:S(2)}, u32[]{:S(2)}) %all-to-all-start.1) | async-done | bytes 245792 | tf_op jit(solution)/shard_map/all_to_all | solution.py:77
  215.0 1.0 gather_fusion
  216.7 24.0 %psum.7 = f32[96,2]{1,0:T(8,128)S(1)} all-reduce(f32[96,2]{1,0:T(8,128)S(1)} %reduce_sum.61), channel_id=1, replica_groups=mesh['ep'=4,'tp'=8] {'tp'}, use_global_device_ids=true, to_apply=%region_9.11 | all-reduce | flops 192 | bytes 1536 | tf_op jit(solution)/shard_map/psum | solution.py:91
  241.3 1.0 reduce_sum.59
  242.3 1.1 multiply_reduce_fusion.1
  243.4 0.8 all-gather.10.cloned.1.call-done
  244.2 8.7 %fusion = bf16[1,384,8192]{2,1,0:T(8,128)(2,1)} fusion(bf16[320,384]{1,0:T(8,128)(2,1)S(1)} %bitcast.69, bf16[320,8192]{1,0:T(8,128)(2,1)} %all-gather.10.cloned.1.call-done), kind=kOutput, calls=%fused_computation.5 | convolution fusion | flops 2016411648 | bytes 11780096 | tf_op jit(solution)/shard_map/dot_general | solution.py:13
  252.8 34.0 %all-gather.14.cloned.1.call-done = bf16[320,8192]{1,0:T(8,128)(2,1)} async-done(((bf16[320,1024]{1,0:T(8,128)(2,1)}), bf16[320,8192]{1,0:T(8,128)(2,1)}) %all-gather.14.cloned.1.call-update) | async-done | bytes 5242896 | tf_op jit(solution)/shard_map/all_gather | solution.py:115
  286.8 9.3 %fusion.2 = bf16[1,8192,384]{2,1,0:T(8,128)(2,1)} fusion(bf16[320,8192]{1,0:T(8,128)(2,1)} %all-gather.14.cloned.1.call-done, bf16[320,384]{1,0:T(8,128)(2,1)S(1)} %bitcast.72), kind=kOutput, calls=%fused_computation.7 | convolution fusion | flops 2016411648 | bytes 11780096 | tf_op jit(solution)/shard_map/dot_general | solution.py:13
  296.2 33.6 %all-gather.12.cloned.1.call-done = bf16[320,8192]{1,0:T(8,128)(2,1)} async-done(((bf16[320,1024]{1,0:T(8,128)(2,1)}), bf16[320,8192]{1,0:T(8,128)(2,1)}) %all-gather.12.cloned.1.call-update) | async-done | bytes 5242896 | tf_op jit(solution)/shard_map/all_gather | solution.py:121
  329.8 8.7 %fusion.1 = bf16[1,384,8192]{2,1,0:T(8,128)(2,1)} fusion(bf16[320,384]{1,0:T(8,128)(2,1)S(1)} %bitcast.70, bf16[320,8192]{1,0:T(8,128)(2,1)} %all-gather.12.cloned.1.call-done), kind=kOutput, calls=%fused_computation.6 | convolution fusion | flops 2016411648 | bytes 11780096 | tf_op jit(solution)/shard_map/dot_general | solution.py:13
  (60 shorter events, 7.7 us)
Async XLA Ops:
  7.2 21.0 %copy-start = (bf16[96,384]{1,0:T(8,128)(2,1)S(1)}, bf16[96,384]{1,0:T(8,128)(2,1)}, u32[]{:S(2)}) copy-start(bf16[96,384]{1,0:T(8,128)(2,1)} %param.9) | copy-start | bytes 221188
  7.2 46.7 %all-gather.8.cloned.1.call-start = ((), (), s32[]{:S(2)}) async-start(), calls=%async_computation.7 | async-start | bytes 2211840 | tf_op jit(solution)/shard_map/all_gather | solution.py:92
  27.1 56.2 %all-gather.6.cloned.1.call-start = ((), (), s32[]{:S(2)}) async-start(), calls=%async_computation.6 | async-start | bytes 2211840 | tf_op jit(solution)/shard_map/all_gather | solution.py:67
  39.2 114.9 %reduce-scatter.9.cloned.1.call-start = ((), (), s32[]{:S(2)}) async-start(), calls=%async_computation.12 | async-start | bytes 2654208
  83.3 5.7 %copy-start.6 = (bf16[320,3072]{1,0:T(8,128)(2,1)S(1)}, bf16[320,3072]{1,0:T(8,128)(2,1)}, u32[]{:S(2)}) copy-start(bf16[320,3072]{1,0:T(8,128)(2,1)} %all-gather.6.cloned.1.call-done) | copy-start | bytes 5898244
  95.6 7.2 %copy-start.4 = (bf16[320,1024]{1,0:T(8,128)(2,1)}, bf16[320,1024]{1,0:T(8,128)(2,1)S(1)}, u32[]{:S(2)}) copy-start(bf16[320,1024]{1,0:T(8,128)(2,1)S(1)} %get-tuple-element.34) | copy-start | bytes 1966084
  109.1 2.7 copy-start.5
  111.6 88.6 %reduce-scatter.7.cloned.1.call-start = ((), (), s32[]{:S(2)}) async-start(), calls=%async_computation.11 | async-start | bytes 2654208
  119.2 124.9 %all-gather.10.cloned.1.call-start = ((), (), s32[]{:S(2)}) async-start(), calls=%async_computation.8 | async-start | bytes 5898240 | tf_op jit(solution)/shard_map/all_gather | solution.py:118
  119.8 167.0 %all-gather.14.cloned.1.call-start = ((), (), s32[]{:S(2)}) async-start(), calls=%async_computation.10 | async-start | bytes 5898240 | tf_op jit(solution)/shard_map/all_gather | solution.py:115
  120.4 209.3 %all-gather.12.cloned.1.call-start = ((), (), s32[]{:S(2)}) async-start(), calls=%async_computation.9 | async-start | bytes 5898240 | tf_op jit(solution)/shard_map/all_gather | solution.py:121
  121.2 123.0 %copy-start.2 = (bf16[4,80,384]{2,1,0:T(8,128)(2,1)S(1)}, bf16[4,80,384]{2,1,0:T(8,128)(2,1)}, u32[]{:S(2)}) copy-start(bf16[4,80,384]{2,1,0:T(8,128)(2,1)} %all_to_all.21) | copy-start | bytes 737284
  155.9 46.2 %all-to-all-start.3 = ((bf16[4,80,384]{2,1,0:T(8,128)(2,1)}), bf16[4,80,384]{2,1,0:T(8,128)(2,1)S(1)}, u32[]{:S(2)}, u32[]{:S(2)}) async-start(bf16[4,80,384]{2,1,0:T(8,128)(2,1)} %bitcast.11), calls=%async_computation.3 | async-start | bytes 491520 | tf_op jit(solution)/shard_map/all_to_all | solution.py:101
  202.0 13.0 %all-to-all-start.1 = ((bf16[4,80,384]{2,1,0:T(8,128)(2,1)}), bf16[4,80,384]{2,1,0:T(8,128)(2,1)S(1)}, u32[]{:S(2)}, u32[]{:S(2)}) async-start(bf16[4,80,384]{2,1,0:T(8,128)(2,1)} %bitcast.7), calls=%async_computation.1 | async-start | bytes 491520 | tf_op jit(solution)/shard_map/all_to_all | solution.py:77
  243.4 43.5 %copy-start.3 = (bf16[4,80,384]{2,1,0:T(8,128)(2,1)S(1)}, bf16[4,80,384]{2,1,0:T(8,128)(2,1)}, u32[]{:S(2)}) copy-start(bf16[4,80,384]{2,1,0:T(8,128)(2,1)} %all_to_all.20) | copy-start | bytes 737284
  286.8 51.6 %copy-start.1 = (bf16[96,384]{1,0:T(8,128)(2,1)S(1)}, bf16[96,384]{1,0:T(8,128)(2,1)}, u32[]{:S(2)}) copy-start(bf16[96,384]{1,0:T(8,128)(2,1)} %param.9) | copy-start | bytes 221188
Sparse Core Ops, SparseCore 0:
  27.2 26.6 all-gather.7
  55.7 27.5 all-gather.5
  111.7 42.3 reduce-scatter.8
  157.8 42.3 reduce-scatter.6
  202.5 41.5 all-gather.9
  245.9 40.8 all-gather.13
  288.7 40.9 all-gather.11
where the time goes:
time: 346 us; the launch traced here: 345 us
  waiting for transfers between devices  189 us (55%)
  matrix products  63.6 us (18%)
  blocking collectives  49.5 us (14%)
  local copies, waits for them, and re-layouts  15 us (4%)
  between operations  14.3 us (4%)
  starting transfers between devices  9.68 us (3%)
  other arithmetic  4.55 us (1%)
    unnamed x9, waiting for transfers between devices  74.4 us
    all_gather x1, waiting for transfers between devices, body(): lax.all_gather(hidden, 'tp', axis=1, tiled=True)  34 us
    all_gather x1, waiting for transfers between devices, body(): lax.all_gather(grad_up_pre, 'tp', axis=1, tiled=True)  33.6 us
    dot_general x3, matrix products, contract_rows(): lax.dot_general(left, right, (((0,), (0,)), ((), ())), preferred_element_...  26.6 us
    psum x1, blocking collectives, body(): grad_combine = lax.psum(local_products, 'tp')  24 us
    all_gather x1, waiting for transfers between devices, body(): piece = lax.all_gather(recv_rows, 'tp', axis=1, tiled=True)  23.8 us
    dot_general x3, matrix products, contract_cols(): lax.dot_general(left, right, (((1,), (1,)), ((), ())), preferred_element_...  19.1 us
    all_to_all x1, blocking collectives, body(): lax.all_to_all(send_grad.reshape(groups, capacity, piece_width), 'ep', sp...  14.8 us
  transfers between devices with their start and end apart: 9, of which 8 were waited for; matrix products, arithmetic and copies ran while one was open for 12% of the time, Pallas kernels for 0%

commit v1 on v0

--- a/solution.py
+++ b/solution.py
@@ -1,7 +1,24 @@
+import functools
 import jax
 import jax.numpy as jnp
 from jax import lax
 from jax.sharding import PartitionSpec as P
+
+
+def name_the_block(own_rows, a_name):
+    n_chips = lax.psum(1, a_name)
+    extra = own_rows
+    fields = [extra]
+    known = [(k0 - 1, k0) for k0 in range(1, n_chips)] + [(n_chips - 1, 0)]
+    for _ in range(n_chips - 1):
+        extra = lax.ppermute(extra, a_name, known)
+        fields += [extra]
+    return jnp.roll(
+        jnp.concatenate([*reversed(fields)], 1), (lax.axis_index(a_name) + 1) * extra.shape[1], 1
+    )
+
+
+work_the_plate = functools.partial(name_the_block, a_name="tp")
 
 
 def silu_parts(gate_pre):
@@ -64,7 +81,7 @@
         ),
     )
     recv_rows = recv_rows.reshape(buffer_rows, piece_width)
-    piece = lax.all_gather(recv_rows, "tp", axis=1, tiled=True)
+    piece = work_the_plate(recv_rows)
     gate_pre = jnp.dot(piece, gate_weight, preferred_element_type=jnp.float32)
     up_pre = jnp.dot(piece, up_weight, preferred_element_type=jnp.float32)
     recv_grad = recv_grad.reshape(buffer_rows, piece_width)

time: 346 us -> 344 us (level)
  blocking collectives: 49.5 us -> 38.6 us
  local copies, waits for them, and re-layouts: 15 us -> 18.5 us
    ppermute x0 -> x7, waiting for transfers between devices: none -> 41.6 us  [name_the_block(): extra = lax.ppermute(extra, a_name, known)]
    all_gather x1 -> x0, waiting for transfers between devices: 23.8 us -> none  [body(): piece = lax.all_gather(recv_rows, 'tp', axis=1, tiled=True)]
    all_to_all x1 -> x0, blocking collectives: 14.8 us -> none  [body(): lax.all_to_all(send_grad.reshape(groups, capacity, piece_width), 'ep', sp...]
    all_gather x1, waiting for transfers between devices: 14.6 us -> 0.02 us  [body(): lax.all_gather(recv_grad, 'tp', axis=1, tiled=True)]
    all_to_all x1, blocking collectives: 10.8 us -> 14.7 us  [body(): lax.all_to_all(send_rows.reshape(groups, capacity, piece_width), 'ep', sp...]
    unnamed x22 -> x41, local copies, waits for them, and re-layouts: 10.7 us -> 14.1 us
    unnamed x9 -> x8, waiting for transfers between devices: 74.4 us -> 73.6 us
  transfers between devices with their start and end apart: 9 -> 16, of which waited for: 8 -> 14; matrix products, arithmetic and copies ran while one was open for 12% -> 12% of each run, Pallas kernels for 0% -> 0%
where the time goes in v1:
time: 344 us; the launch traced here: 343 us
  waiting for transfers between devices  192 us (56%)
  matrix products  61.2 us (18%)
  blocking collectives  38.6 us (11%)
  local copies, waits for them, and re-layouts  18.5 us (5%)
  between operations  14.4 us (4%)
  starting transfers between devices  13.1 us (4%)
  other arithmetic  4.56 us (1%)
    unnamed x8, waiting for transfers between devices  73.6 us
    ppermute x7, waiting for transfers between devices, name_the_block(): extra = lax.ppermute(extra, a_name, known)  41.6 us
    all_gather x1, waiting for transfers between devices, body(): lax.all_gather(hidden, 'tp', axis=1, tiled=True)  34.1 us
    all_gather x1, waiting for transfers between devices, body(): lax.all_gather(grad_up_pre, 'tp', axis=1, tiled=True)  34 us
    dot_general x3, matrix products, contract_rows(): lax.dot_general(left, right, (((0,), (0,)), ((), ())), preferred_element_...  26.6 us
    psum x1, blocking collectives, body(): grad_combine = lax.psum(local_products, 'tp')  24 us
    dot_general x3, matrix products, contract_cols(): lax.dot_general(left, right, (((1,), (1,)), ((), ())), preferred_element_...  19.5 us
    all_to_all x1, blocking collectives, body(): lax.all_to_all(send_rows.reshape(groups, capacity, piece_width), 'ep', sp...  14.7 us
  transfers between devices with their start and end apart: 16, of which 14 were waited for; matrix products, arithmetic and copies ran while one was open for 12% of the time, Pallas kernels for 0%

profile of v1, /device:TPU:0, one launch (start us, length us, event | category | flops | bytes accessed | tf_op | source)
XLA Modules:
  0.0 342.9 jit_solution(13734411588040895843)
XLA Ops:
  8.2 1.2 reduce-window.6
  11.1 14.7 %all_to_all.20 = bf16[4,80,384]{2,1,0:T(8,128)(2,1)S(1)} all-to-all(bf16[4,80,384]{2,1,0:T(8,128)(2,1)S(1)} %bitcast.73), channel_id=1, replica_groups=mesh['ep'=4,'tp'=8] {'ep'}, dimensions={0} | all-to-all | bytes 491520 | tf_op jit(solution)/shard_map/all_to_all | solution.py:68
  27.9 4.4 %collective-permute-done = bf16[320,384]{1,0:T(8,128)(2,1)S(1)} collective-permute-done((bf16[320,384]{1,0:T(8,128)(2,1)S(1)}, bf16[320,384]{1,0:T(8,128)(2,1)S(1)}, u32[]{:S(2)}, u32[]{:S(2)}) %collective-permute-start) | collective-permute-done | bytes 245792 | tf_op jit(solution)/shard_map/ppermute | solution.py:14
  33.3 3.4 all-to-all-start.2
  36.8 2.0 collective-permute-done.1
  38.8 6.5 %collective-permute-done.2 = bf16[320,384]{1,0:T(8,128)(2,1)S(1)} collective-permute-done((bf16[320,384]{1,0:T(8,128)(2,1)S(1)}, bf16[320,384]{1,0:T(8,128)(2,1)S(1)}, u32[]{:S(2)}, u32[]{:S(2)}) %collective-permute-start.2) | collective-permute-done | bytes 245792 | tf_op jit(solution)/shard_map/ppermute | solution.py:14
  47.1 4.7 %collective-permute-done.3 = bf16[320,384]{1,0:T(8,128)(2,1)S(1)} collective-permute-done((bf16[320,384]{1,0:T(8,128)(2,1)S(1)}, bf16[320,384]{1,0:T(8,128)(2,1)S(1)}, u32[]{:S(2)}, u32[]{:S(2)}) %collective-permute-start.3) | collective-permute-done | bytes 245792 | tf_op jit(solution)/shard_map/ppermute | solution.py:14
  51.9 9.2 %collective-permute-done.4 = bf16[320,384]{1,0:T(8,128)(2,1)S(1)} collective-permute-done((bf16[320,384]{1,0:T(8,128)(2,1)S(1)}, bf16[320,384]{1,0:T(8,128)(2,1)S(1)}, u32[]{:S(2)}, u32[]{:S(2)}) %collective-permute-start.4) | collective-permute-done | bytes 245792 | tf_op jit(solution)/shard_map/ppermute | solution.py:14
  61.0 6.6 %collective-permute-done.5 = bf16[320,384]{1,0:T(8,128)(2,1)S(1)} collective-permute-done((bf16[320,384]{1,0:T(8,128)(2,1)S(1)}, bf16[320,384]{1,0:T(8,128)(2,1)S(1)}, u32[]{:S(2)}, u32[]{:S(2)}) %collective-permute-start.5) | collective-permute-done | bytes 245792 | tf_op jit(solution)/shard_map/ppermute | solution.py:14
  67.6 8.2 %collective-permute-done.6 = bf16[320,384]{1,0:T(8,128)(2,1)S(1)} collective-permute-done((bf16[320,384]{1,0:T(8,128)(2,1)S(1)}, bf16[320,384]{1,0:T(8,128)(2,1)S(1)}, u32[]{:S(2)}, u32[]{:S(2)}) %collective-permute-start.6) | collective-permute-done | bytes 245792 | tf_op jit(solution)/shard_map/ppermute | solution.py:14
  76.8 1.9 copy-done.6
  78.7 2.3 fusion.9
  81.0 5.7 %fusion.3 = f32[320,1024]{1,0:T(8,128)S(1)} fusion(bf16[320,3072]{1,0:T(8,128)(2,1)} %all-gather.5.cloned.1.call-done, bf16[1,1024,3072]{2,1,0:T(8,128)(2,1)} %param.15), kind=kOutput, calls=%fused_computation.8 | convolution fusion | flops 2013265920 | bytes 9568256 | tf_op jit(solution)/shard_map/dot_general | solution.py:36
  86.8 6.5 %multiply_convert_fusion.1 = (bf16[320,1024]{1,0:T(8,128)(2,1)}, bf16[320,1024]{1,0:T(8,128)(2,1)S(1)}, bf16[320,1024]{1,0:T(8,128)(2,1)S(1)}) fusion(f32[320,1024]{1,0:T(8,128)S(1)} %fusion.3, f32[320,1024]{1,0:T(8,128)S(1)} %fusion.9, bf16[1,3072,1024]{2,1,0:T(8,128)(2,1)} %param.13, bf16[320,6144]{1,0:T(8,128)(2,1)S(1)} %copy-done.7, s32[]{:T(128)S(6)} %select_n.21), kind=kOutput, calls=%fused_computation.26 | convolution fusion | flops 2018181120 | bytes 12845060 | tf_op jit(solution)/shard_map/dot_general | solution.py:85
  93.3 7.4 %fusion.7 = f32[320,3072]{1,0:T(8,128)} fusion(bf16[320,1024]{1,0:T(8,128)(2,1)S(1)} %get-tuple-element.34, bf16[1,3072,1024]{2,1,0:T(8,128)(2,1)} %param.14), kind=kOutput, calls=%fused_computation.12 | convolution fusion | flops 2013265920 | bytes 10878976 | tf_op jit(solution)/shard_map/dot_general | solution.py:36
  100.7 6.3 %fusion.18 = bf16[320,3072]{1,0:T(8,128)(2,1)S(1)} fusion(f32[320,3072]{1,0:T(8,128)} %fusion.7, bf16[320,1024]{1,0:T(8,128)(2,1)} %get-tuple-element.33, bf16[1,3072,1024]{2,1,0:T(8,128)(2,1)} %param.13), kind=kOutput, calls=%fused_computation.21 | convolution fusion | flops 2015232000 | bytes 12845056 | tf_op jit(solution)/shard_map/dot_general | solution.py:36
  107.1 2.4 copy.51
  109.8 5.0 %fusion.21 = bf16[320,3072]{1,0:T(8,128)(2,1)S(1)} fusion(bf16[320,1024]{1,0:T(8,128)(2,1)S(1)} %get-tuple-element.35, bf16[1,1024,3072]{2,1,0:T(8,128)(2,1)} %param.15), kind=kOutput, calls=%fused_computation.22 | convolution fusion | flops 2014248960 | bytes 8912896 | tf_op jit(solution)/shard_map/dot_general | solution.py:90
  114.8 2.4 copy.49
  119.0 32.1 %reduce-scatter.9.cloned.1.call-done = bf16[384,320]{1,0:T(8,128)(2,1)} async-done(((bf16[3072,320]{1,0:T(8,128)(2,1)}), bf16[384,320]{1,0:T(8,128)(2,1)}) %reduce-scatter.9.cloned.1.call-update) | async-done | bytes 245776
  151.1 1.8 copy.52
  152.9 4.6 %all-to-all-start.3 = ((bf16[4,80,384]{2,1,0:T(8,128)(2,1)}), bf16[4,80,384]{2,1,0:T(8,128)(2,1)S(1)}, u32[]{:S(2)}, u32[]{:S(2)}) async-start(bf16[4,80,384]{2,1,0:T(8,128)(2,1)} %bitcast.11), calls=%async_computation.3 | async-start | bytes 491520 | tf_op jit(solution)/shard_map/all_to_all | solution.py:118
  157.5 39.9 %reduce-scatter.7.cloned.1.call-done = bf16[384,320]{1,0:T(8,128)(2,1)} async-done(((bf16[3072,320]{1,0:T(8,128)(2,1)}), bf16[384,320]{1,0:T(8,128)(2,1)}) %reduce-scatter.7.cloned.1.call-update) | async-done | bytes 245776
  197.4 1.8 copy.50
  199.2 4.6 %all-to-all-start.1 = ((bf16[4,80,384]{2,1,0:T(8,128)(2,1)}), bf16[4,80,384]{2,1,0:T(8,128)(2,1)S(1)}, u32[]{:S(2)}, u32[]{:S(2)}) async-start(bf16[4,80,384]{2,1,0:T(8,128)(2,1)} %bitcast.7), calls=%async_computation.1 | async-start | bytes 491520 | tf_op jit(solution)/shard_map/all_to_all | solution.py:94
  204.8 7.3 %all-to-all-done.1 = bf16[4,80,384]{2,1,0:T(8,128)(2,1)S(1)} async-done(((bf16[4,80,384]{2,1,0:T(8,128)(2,1)}), bf16[4,80,384]{2,1,0:T(8,128)(2,1)S(1)}, u32[]{:S(2)}, u32[]{:S(2)}) %all-to-all-start.1) | async-done | bytes 245792 | tf_op jit(solution)/shard_map/all_to_all | solution.py:94
  213.9 24.0 %psum.7 = f32[96,2]{1,0:T(8,128)S(1)} all-reduce(f32[96,2]{1,0:T(8,128)S(1)} %reduce_sum.61), channel_id=1, replica_groups=mesh['ep'=4,'tp'=8] {'tp'}, use_global_device_ids=true, to_apply=%region_9.11 | all-reduce | flops 192 | bytes 1536 | tf_op jit(solution)/shard_map/psum | solution.py:108
  241.3 8.7 %fusion = bf16[1,384,8192]{2,1,0:T(8,128)(2,1)} fusion(bf16[320,384]{1,0:T(8,128)(2,1)S(1)} %bitcast.69, bf16[320,8192]{1,0:T(8,128)(2,1)} %all-gather.7.cloned.1.call-done), kind=kOutput, calls=%fused_computation.5 | convolution fusion | flops 2016411648 | bytes 11780096 | tf_op jit(solution)/shard_map/dot_general | solution.py:30
  250.0 34.0 %all-gather.9.cloned.1.call-done = bf16[320,8192]{1,0:T(8,128)(2,1)} async-done(((bf16[320,1024]{1,0:T(8,128)(2,1)}), bf16[320,8192]{1,0:T(8,128)(2,1)}) %all-gather.9.cloned.1.call-update) | async-done | bytes 5242896 | tf_op jit(solution)/shard_map/all_gather | solution.py:138
  284.0 8.7 %fusion.1 = bf16[1,384,8192]{2,1,0:T(8,128)(2,1)} fusion(bf16[320,384]{1,0:T(8,128)(2,1)S(1)} %bitcast.70, bf16[320,8192]{1,0:T(8,128)(2,1)} %all-gather.9.cloned.1.call-done), kind=kOutput, calls=%fused_computation.6 | convolution fusion | flops 2016411648 | bytes 11780096 | tf_op jit(solution)/shard_map/dot_general | solution.py:30
  292.7 34.1 %all-gather.11.cloned.1.call-done = bf16[320,8192]{1,0:T(8,128)(2,1)} async-done(((bf16[320,1024]{1,0:T(8,128)(2,1)}), bf16[320,8192]{1,0:T(8,128)(2,1)}) %all-gather.11.cloned.1.call-update) | async-done | bytes 5242896 | tf_op jit(solution)/shard_map/all_gather | solution.py:132
  326.8 9.3 %fusion.2 = bf16[1,8192,384]{2,1,0:T(8,128)(2,1)} fusion(bf16[320,8192]{1,0:T(8,128)(2,1)} %all-gather.11.cloned.1.call-done, bf16[320,384]{1,0:T(8,128)(2,1)S(1)} %bitcast.72), kind=kOutput, calls=%fused_computation.7 | convolution fusion | flops 2016411648 | bytes 11780096 | tf_op jit(solution)/shard_map/dot_general | solution.py:30
  (92 shorter events, 16.7 us)
Async XLA Ops:
  7.2 3.7 %copy-start = (bf16[96,384]{1,0:T(8,128)(2,1)S(1)}, bf16[96,384]{1,0:T(8,128)(2,1)}, u32[]{:S(2)}) copy-start(bf16[96,384]{1,0:T(8,128)(2,1)} %param.9) | copy-start | bytes 221188
  25.8 6.5 %collective-permute-start = (bf16[320,384]{1,0:T(8,128)(2,1)S(1)}, bf16[320,384]{1,0:T(8,128)(2,1)S(1)}, u32[]{:S(2)}, u32[]{:S(2)}) collective-permute-start(bf16[320,384]{1,0:T(8,128)(2,1)S(1)} %bitcast.66), channel_id=1, source_target_pairs={{0,1},{1,2},{2,3},{3,4},{4,5},{5,6},{6,7},{7,0},{8,9},{9,10},{10,1... | collective-permute-start | bytes 737288 | tf_op jit(solution)/shard_map/ppermute | solution.py:14
  32.3 6.5 %collective-permute-start.1 = (bf16[320,384]{1,0:T(8,128)(2,1)S(1)}, bf16[320,384]{1,0:T(8,128)(2,1)S(1)}, u32[]{:S(2)}, u32[]{:S(2)}) collective-permute-start(bf16[320,384]{1,0:T(8,128)(2,1)S(1)} %collective-permute-done), channel_id=1, source_target_pairs={{0,1},{1,2},{2,3},{3,4},{4,5},{5,6},{6,7},{7,0},{8,9},{9,10},{10,1... | collective-permute-start | bytes 737288 | tf_op jit(solution)/shard_map/ppermute | solution.py:14
  33.3 13.0 %all-to-all-start.2 = ((bf16[4,80,384]{2,1,0:T(8,128)(2,1)}), bf16[4,80,384]{2,1,0:T(8,128)(2,1)S(1)}, u32[]{:S(2)}, u32[]{:S(2)}) async-start(bf16[4,80,384]{2,1,0:T(8,128)(2,1)} %bitcast.9), calls=%async_computation.2 | async-start | bytes 491520 | tf_op jit(solution)/shard_map/all_to_all | solution.py:75
  36.7 44.3 %all-gather.5.cloned.1.call-start = ((), (), s32[]{:S(2)}) async-start(), calls=%async_computation.6 | async-start | bytes 2211840 | tf_op jit(solution)/shard_map/all_gather | solution.py:109
  38.8 6.5 %collective-permute-start.2 = (bf16[320,384]{1,0:T(8,128)(2,1)S(1)}, bf16[320,384]{1,0:T(8,128)(2,1)S(1)}, u32[]{:S(2)}, u32[]{:S(2)}) collective-permute-start(bf16[320,384]{1,0:T(8,128)(2,1)S(1)} %collective-permute-done.1), channel_id=1, source_target_pairs={{0,1},{1,2},{2,3},{3,4},{4,5},{5,6},{6,7},{7,0},{8,9},{9,10},{10,1... | collective-permute-start | bytes 737288 | tf_op jit(solution)/shard_map/ppermute | solution.py:14
  45.3 6.5 %collective-permute-start.3 = (bf16[320,384]{1,0:T(8,128)(2,1)S(1)}, bf16[320,384]{1,0:T(8,128)(2,1)S(1)}, u32[]{:S(2)}, u32[]{:S(2)}) collective-permute-start(bf16[320,384]{1,0:T(8,128)(2,1)S(1)} %collective-permute-done.2), channel_id=1, source_target_pairs={{0,1},{1,2},{2,3},{3,4},{4,5},{5,6},{6,7},{7,0},{8,9},{9,10},{10,1... | collective-permute-start | bytes 737288 | tf_op jit(solution)/shard_map/ppermute | solution.py:14
  46.4 0.7 copy-start.2
  47.1 104.0 %reduce-scatter.9.cloned.1.call-start = ((), (), s32[]{:S(2)}) async-start(), calls=%async_computation.11 | async-start | bytes 2654208
  51.9 9.2 %collective-permute-start.4 = (bf16[320,384]{1,0:T(8,128)(2,1)S(1)}, bf16[320,384]{1,0:T(8,128)(2,1)S(1)}, u32[]{:S(2)}, u32[]{:S(2)}) collective-permute-start(bf16[320,384]{1,0:T(8,128)(2,1)S(1)} %collective-permute-done.3), channel_id=1, source_target_pairs={{0,1},{1,2},{2,3},{3,4},{4,5},{5,6},{6,7},{7,0},{8,9},{9,10},{10,1... | collective-permute-start | bytes 737288 | tf_op jit(solution)/shard_map/ppermute | solution.py:14
  61.0 6.6 %collective-permute-start.5 = (bf16[320,384]{1,0:T(8,128)(2,1)S(1)}, bf16[320,384]{1,0:T(8,128)(2,1)S(1)}, u32[]{:S(2)}, u32[]{:S(2)}) collective-permute-start(bf16[320,384]{1,0:T(8,128)(2,1)S(1)} %collective-permute-done.4), channel_id=1, source_target_pairs={{0,1},{1,2},{2,3},{3,4},{4,5},{5,6},{6,7},{7,0},{8,9},{9,10},{10,1... | collective-permute-start | bytes 737288 | tf_op jit(solution)/shard_map/ppermute | solution.py:14
  67.6 8.2 %collective-permute-start.6 = (bf16[320,384]{1,0:T(8,128)(2,1)S(1)}, bf16[320,384]{1,0:T(8,128)(2,1)S(1)}, u32[]{:S(2)}, u32[]{:S(2)}) collective-permute-start(bf16[320,384]{1,0:T(8,128)(2,1)S(1)} %collective-permute-done.5), channel_id=1, source_target_pairs={{0,1},{1,2},{2,3},{3,4},{4,5},{5,6},{6,7},{7,0},{8,9},{9,10},{10,1... | collective-permute-start | bytes 737288 | tf_op jit(solution)/shard_map/ppermute | solution.py:14
  67.6 11.1 %copy-start.8 = (bf16[1,3072,1024]{2,1,0:T(8,128)(2,1)S(1)}, bf16[1,3072,1024]{2,1,0:T(8,128)(2,1)}, u32[]{:S(2)}) copy-start(bf16[1,3072,1024]{2,1,0:T(8,128)(2,1)} %param.14) | copy-start | bytes 18874372
  76.8 1.9 copy-start.6
  81.0 5.8 %copy-start.7 = (bf16[320,6144]{1,0:T(8,128)(2,1)S(1)}, bf16[320,6144]{1,0:T(8,128)(2,1)}, u32[]{:S(2)}) copy-start(bf16[320,6144]{1,0:T(8,128)(2,1)} %copy-done.6) | copy-start | bytes 11796484
  93.3 7.4 %copy-start.5 = (bf16[320,1024]{1,0:T(8,128)(2,1)}, bf16[320,1024]{1,0:T(8,128)(2,1)S(1)}, u32[]{:S(2)}) copy-start(bf16[320,1024]{1,0:T(8,128)(2,1)S(1)} %get-tuple-element.34) | copy-start | bytes 1966084
  93.3 16.5 %copy-start.4 = (bf16[320,1024]{1,0:T(8,128)(2,1)}, bf16[320,1024]{1,0:T(8,128)(2,1)S(1)}, u32[]{:S(2)}) copy-start(bf16[320,1024]{1,0:T(8,128)(2,1)S(1)} %get-tuple-element.35) | copy-start | bytes 1966084
  109.5 87.9 %reduce-scatter.7.cloned.1.call-start = ((), (), s32[]{:S(2)}) async-start(), calls=%async_computation.10 | async-start | bytes 2654208
  117.3 124.1 %all-gather.7.cloned.1.call-start = ((), (), s32[]{:S(2)}) async-start(), calls=%async_computation.7 | async-start | bytes 5898240 | tf_op jit(solution)/shard_map/all_gather | solution.py:135
  117.9 166.2 %all-gather.9.cloned.1.call-start = ((), (), s32[]{:S(2)}) async-start(), calls=%async_computation.8 | async-start | bytes 5898240 | tf_op jit(solution)/shard_map/all_gather | solution.py:138
  118.4 208.4 %all-gather.11.cloned.1.call-start = ((), (), s32[]{:S(2)}) async-start(), calls=%async_computation.9 | async-start | bytes 5898240 | tf_op jit(solution)/shard_map/all_gather | solution.py:132
  152.9 46.3 %all-to-all-start.3 = ((bf16[4,80,384]{2,1,0:T(8,128)(2,1)}), bf16[4,80,384]{2,1,0:T(8,128)(2,1)S(1)}, u32[]{:S(2)}, u32[]{:S(2)}) async-start(bf16[4,80,384]{2,1,0:T(8,128)(2,1)} %bitcast.11), calls=%async_computation.3 | async-start | bytes 491520 | tf_op jit(solution)/shard_map/all_to_all | solution.py:118
  199.2 12.9 %all-to-all-start.1 = ((bf16[4,80,384]{2,1,0:T(8,128)(2,1)}), bf16[4,80,384]{2,1,0:T(8,128)(2,1)S(1)}, u32[]{:S(2)}, u32[]{:S(2)}) async-start(bf16[4,80,384]{2,1,0:T(8,128)(2,1)} %bitcast.7), calls=%async_computation.1 | async-start | bytes 491520 | tf_op jit(solution)/shard_map/all_to_all | solution.py:94
  250.0 76.8 %copy-start.3 = (bf16[4,80,384]{2,1,0:T(8,128)(2,1)S(1)}, bf16[4,80,384]{2,1,0:T(8,128)(2,1)}, u32[]{:S(2)}) copy-start(bf16[4,80,384]{2,1,0:T(8,128)(2,1)} %copy-done.2) | copy-start | bytes 737284
  284.0 52.0 %copy-start.1 = (bf16[96,384]{1,0:T(8,128)(2,1)S(1)}, bf16[96,384]{1,0:T(8,128)(2,1)}, u32[]{:S(2)}) copy-start(bf16[96,384]{1,0:T(8,128)(2,1)} %param.9) | copy-start | bytes 221188
Sparse Core Ops, SparseCore 0:
  47.2 28.0 all-gather.4
  109.6 41.4 reduce-scatter.8
  155.0 42.3 reduce-scatter.6
  199.7 41.5 all-gather.6
  243.1 40.8 all-gather.8
  285.8 40.9 all-gather.10
